TPU v7x, 32 devices: a whole 2x2x4 slice. The times are simulated.
32 devices in a mesh: dp: 8 (over y, x, core), mp: 4 (over z).
Axes of the slice: x: 2, y: 2, z: 4, core: 2. Of those that a mesh axis runs over, the one named last changes fastest.
Arguments:
- activations: bfloat16 [8192, 4096], P(('dp', 'mp')), may hold values from -17 to 17
- output_grads: bfloat16 [8192, 14336], P('dp', 'mp'), may hold values from -0.046875 to 0.046875
- q_start: float32 [14336, 64], P('mp'), may hold values from -6 to 6
Outputs:
- new_error: bfloat16 [32768, 14336], P('dp', 'mp')
- q_factor: float32 [14336, 64], P('mp')
All inputs are finite; a program needn't handle non-finite values.
Results may differ from a plain program's by a relative error of at most 0.01.
Values may be sent and summed in bfloat16 or wider, within the bound.
A program may use at most 192 MiB of HBM per device.

v0:
```python
import functools

import jax
import jax.numpy as jnp
from jax import lax
from jax.experimental import pallas as pl
from jax.experimental.pallas import tpu as pltpu
from jax.sharding import PartitionSpec as P

ROWS = (((0,), (0,)), ((), ()))
COLS = (((1,), (1,)), ((), ()))
MESH = pl.DeviceIdType.MESH
F32 = jnp.float32
BF16 = jnp.bfloat16
CHUNKS = 16
EARLY = 11


def split_parts(values):
    upper = values.astype(BF16)
    lower = (values - upper.astype(F32)).astype(BF16)
    return (upper, lower)


def inverse_factor(gram):
    rank = gram.shape[0]
    row = lax.broadcasted_iota(jnp.int32, (rank, rank), 0)
    col = lax.broadcasted_iota(jnp.int32, (rank, rank), 1)
    left = gram
    right = jnp.where(row == col, 1.0, 0.0).astype(F32)
    down = lax.broadcasted_iota(jnp.int32, (rank, 1), 0)
    pivots = jnp.ones((rank, 1), F32)
    for k in range(rank):
        pivot = left[k : k + 1, k : k + 1]
        pivots = jnp.where(down == k, pivot, pivots)
        factor = jnp.where(down > k, left[:, k : k + 1] / pivot, 0.0)
        left_row = left[k : k + 1, :]
        right_row = right[k : k + 1, :]
        left = left - factor * left_row
        right = right - factor * right_row
    return right / jnp.sqrt(pivots)


class Exchange:
    def __init__(self, axis, count, me, source, target, send_sem, recv_sem):
        self.copies = []
        for shift in range(1, count):
            peer = lax.rem(me + shift, count)
            self.copies.append(
                pltpu.make_async_remote_copy(
                    src_ref=source(peer),
                    dst_ref=target,
                    send_sem=send_sem.at[shift],
                    recv_sem=recv_sem.at[shift],
                    device_id={axis: peer},
                    device_id_type=MESH,
                )
            )

    def start(self):
        for copy in self.copies:
            copy.start()

    def wait(self):
        for copy in self.copies:
            copy.wait()


def step_kernel(
    dims,
    x_hbm,
    y_hbm,
    q_ref,
    e_ref,
    q_out,
    xg,
    yv,
    xt,
    zpart,
    zrecv,
    part,
    recv,
    full,
    pmat,
    psum,
    pzr,
    pz,
    wall,
    local_sem,
    zs_sem,
    zr_sem,
    ps_sem,
    pr_sem,
    pzs_sem,
    pzr_sem,
    ags_sem,
    agr_sem,
    pgs_sem,
    pgr_sem,
    ws_sem,
    wr_sem,
    us_sem,
    ur_sem,
    uas_sem,
    uar_sem,
    right_send,
    right_recv,
    left_send,
    left_recv,
):
    replicas, shards = dims
    me = lax.axis_index("mp")
    rep = lax.axis_index("dp")
    tokens, depth = x_hbm.shape
    gathered, width = y_hbm.shape
    rank = q_ref.shape[1]
    lines = rank // replicas
    span = depth // shards
    chunk = depth // CHUNKS
    highest = lax.Precision.HIGHEST
    mine = pl.ds(pl.multiple_of(me * tokens, tokens), tokens)

    x_copy = pltpu.make_async_copy(x_hbm, xg.at[mine, :], local_sem.at[0])
    y_copy = pltpu.make_async_copy(y_hbm, yv.at[pl.ds(0, gathered), :], local_sem.at[1])
    x_copy.start()
    y_copy.start()

    barrier = pltpu.get_barrier_semaphore()
    for shift in range(1, shards):
        peer = lax.rem(me + shift, shards)
        pl.semaphore_signal(barrier, inc=1, device_id={"mp": peer}, device_id_type=MESH)
    for shift in range(1, replicas):
        peer = lax.rem(rep + shift, replicas)
        pl.semaphore_signal(barrier, inc=1, device_id={"dp": peer}, device_id_type=MESH)
    pl.semaphore_wait(barrier, shards + replicas - 2)

    def hop(owner, c, send_sem, recv_sem, target):
        rows = pl.ds(pl.multiple_of(owner * tokens, tokens), tokens)
        cols = pl.ds(pl.multiple_of(c * chunk, chunk), chunk)
        block = xg.at[rows, cols]
        return pltpu.make_async_remote_copy(
            src_ref=block,
            dst_ref=block,
            send_sem=send_sem,
            recv_sem=recv_sem,
            device_id={"mp": target},
            device_id_type=MESH,
        )

    def relay(step):
        for h in range(shards):
            c = step - h
            inside = jnp.logical_and(c >= 0, c < CHUNKS)
            for ahead, sends, recvs in ((True, right_send, right_recv), (False, left_send, left_recv)):
                owner = me - h if ahead else me + h
                exists = owner >= 0 if ahead else owner < shards
                onward = me < shards - 1 if ahead else me > 0
                target = me + 1 if ahead else me - 1
                source = me - 1 if ahead else me + 1
                if h >= 1:

                    @pl.when(jnp.logical_and(inside, exists))
                    def _():
                        hop(owner, c, sends.at[h - 1, c], recvs.at[h - 1, c], source).wait_recv()

                if h < shards - 1:

                    @pl.when(jnp.logical_and(inside, jnp.logical_and(exists, onward)))
                    def _():
                        hop(owner, c, sends.at[h, c], recvs.at[h, c], target).start()

    x_copy.wait()
    relay(0)

    q_cat = jnp.concatenate(split_parts(q_ref[...]), axis=1)
    zero_rows = xg.shape[0] - gathered - 3 * rank
    xg[pl.ds(gathered + 3 * rank, zero_rows), :] = jnp.zeros((zero_rows, depth), BF16)
    yv[pl.ds(gathered + 3 * rank, zero_rows), :] = jnp.zeros((zero_rows, width), BF16)
    y_copy.wait()
    both = jnp.dot(yv[pl.ds(0, gathered), :], q_cat, preferred_element_type=F32)
    both = both.T
    projected = both[:rank] + both[rank:]
    for j in range(shards):
        zpart[j] = projected[:, j * tokens : (j + 1) * tokens]
    z_move = Exchange("mp", shards, me, lambda peer: zpart.at[peer], zrecv.at[me], zs_sem, zr_sem)
    z_move.start()
    relay(1)
    z_move.wait()
    total = zpart[me]
    for shift in range(1, shards):
        total = total + zrecv[lax.rem(me + shift, shards)]

    z_cat = jnp.concatenate(split_parts(total), axis=0)
    both = jnp.dot(z_cat, xg[mine, :], preferred_element_type=F32)
    left = both[:rank] + both[rank:]
    for i in range(replicas):
        part[i] = left[i * lines : (i + 1) * lines, :]
    p_move = Exchange("dp", replicas, rep, lambda peer: part.at[peer], recv.at[rep], ps_sem, pr_sem)
    p_move.start()
    relay(2)
    p_move.wait()
    total = part[rep]
    for shift in range(1, replicas):
        total = total + recv[lax.rem(rep + shift, replicas)]
    for j in range(shards):
        psum[j] = total[:, j * span : (j + 1) * span]
    pz_move = Exchange("mp", shards, me, lambda peer: psum.at[peer], pzr.at[me], pzs_sem, pzr_sem)
    pz_move.start()
    relay(3)
    pz_move.wait()
    total = psum[me]
    for shift in range(1, shards):
        total = total + pzr[lax.rem(me + shift, shards)]
    pz[me] = total / replicas
    ag_move = Exchange("mp", shards, me, lambda peer: pz.at[me], pz.at[me], ags_sem, agr_sem)
    ag_move.start()
    relay(4)
    ag_move.wait()
    for j in range(shards):
        full[rep, :, pl.ds(j * span, span)] = pz[j]
    pg_move = Exchange("dp", replicas, rep, lambda peer: full.at[rep], full.at[rep], pgs_sem, pgr_sem)
    pg_move.start()
    relay(5)
    pg_move.wait()
    for i in range(replicas):
        pmat[pl.ds(i * lines, lines), :] = full[i]
    relay(6)

    p_mean = pmat[...]
    gram = lax.dot_general(p_mean, p_mean, COLS, precision=highest, preferred_element_type=F32)
    inverse = inverse_factor(gram)
    ortho = jnp.dot(inverse, pmat[...], precision=highest, preferred_element_type=F32)
    upper, lower = split_parts(-ortho)
    xg[pl.ds(gathered, rank), :] = upper
    xg[pl.ds(gathered + rank, rank), :] = upper
    xg[pl.ds(gathered + 2 * rank, rank), :] = lower
    relay(7)

    both = lax.dot_general(
        xg[pl.ds(gathered + rank, 2 * rank), :], xg[mine, :], COLS, preferred_element_type=F32
    )
    wall[me] = -(both[:rank] + both[rank:])
    w_move = Exchange("mp", shards, me, lambda peer: wall.at[me], wall.at[me], ws_sem, wr_sem)
    w_move.start()
    relay(8)
    w_move.wait()
    seen = jnp.concatenate([wall[j] for j in range(shards)], axis=1)
    w_cat = jnp.concatenate(split_parts(seen), axis=0)
    both = jnp.dot(w_cat, yv[pl.ds(0, gathered), :], preferred_element_type=F32)
    right = both[:rank] + both[rank:]
    used = pl.ds(0, width)
    for i in range(replicas):
        part[i, :, used] = right[i * lines : (i + 1) * lines, :]
    u_move = Exchange(
        "dp", replicas, rep, lambda peer: part.at[peer, :, used], recv.at[rep, :, used], us_sem, ur_sem
    )
    u_move.start()
    relay(9)
    u_move.wait()
    total = part[rep, :, used]
    for shift in range(1, replicas):
        total = total + recv[lax.rem(rep + shift, replicas), :, used]
    full[rep, :, used] = total / replicas
    ua_move = Exchange(
        "dp", replicas, rep, lambda peer: full.at[rep, :, used], full.at[rep, :, used], uas_sem, uar_sem
    )
    ua_move.start()
    relay(10)
    ua_move.wait()
    for i in range(replicas):
        pmat[pl.ds(i * lines, lines), used] = full[i, :, used]
    q_mean = pmat[:, used]
    q_out[...] = q_mean
    upper, lower = split_parts(q_mean)
    yv[pl.ds(gathered, rank), :] = upper
    yv[pl.ds(gathered + rank, rank), :] = lower
    yv[pl.ds(gathered + 2 * rank, rank), :] = upper

    tall = xt.shape[0]
    wide = 512 if width % 512 == 0 else 256

    def tile(t):
        rows = pl.ds(pl.multiple_of(t * tall, tall), tall)
        xt[...] = xg[:, rows].T

        def column(n, carry):
            cols = pl.ds(pl.multiple_of(n * wide, wide), wide)
            e_ref[rows, cols] = jnp.dot(
                xt[...], yv[:, cols], preferred_element_type=F32
            ).astype(BF16)
            return carry

        lax.fori_loop(0, width // wide, column, 0)

    tiles = depth // tall
    each = tall // chunk
    last = CHUNKS + shards - 1
    start = last - tiles

    def late(step, carry):
        relay(step)
        return carry

    lax.fori_loop(EARLY, max(start, EARLY), late, 0)

    def finish(t, carry):
        tile(t)
        step = t + max(start, EARLY)

        @pl.when(step < last)
        def _():
            relay(step)

        return carry

    safe = min(tiles, max(start, EARLY) and tiles - 1)
    lax.fori_loop(0, safe, finish, 0)
    for step in range(safe + max(start, EARLY), last):
        relay(step)
    for t in range(safe, tiles):
        tile(t)

    def drain(c, carry):
        for h in range(shards - 1):

            @pl.when(jnp.logical_and(me - h >= 0, me < shards - 1))
            def _():
                hop(me - h, c, right_send.at[h, c], right_recv.at[h, c], me + 1).wait_send()

            @pl.when(jnp.logical_and(me + h < shards, me > 0))
            def _():
                hop(me + h, c, left_send.at[h, c], left_recv.at[h, c], me - 1).wait_send()

        return carry

    lax.fori_loop(0, CHUNKS, drain, 0)


def write_kernel(error_ref, q_ref, error_out, q_out, sem):
    parts = sem.shape[0]
    rows = error_ref.shape[0] // parts
    copies = []
    for k in range(parts):
        here = pl.ds(k * rows, rows)
        copies.append(
            pltpu.make_async_copy(error_ref.at[here, :], error_out.at[here, :], sem.at[k])
        )
        copies[-1].start()
    q_out[...] = q_ref[...].T
    for copy in copies:
        copy.wait()


def write_out(error, q_mean):
    depth, width = error.shape
    vmem = pl.BlockSpec(memory_space=pltpu.VMEM)
    return pl.pallas_call(
        write_kernel,
        out_shape=(
            jax.ShapeDtypeStruct((depth, width), error.dtype),
            jax.ShapeDtypeStruct((width, q_mean.shape[0]), q_mean.dtype),
        ),
        in_specs=[vmem, vmem],
        out_specs=(pl.BlockSpec(memory_space=pl.ANY), vmem),
        scratch_shapes=[pltpu.SemaphoreType.DMA((8,))],
        compiler_params=pltpu.CompilerParams(vmem_limit_bytes=8 * 2**20),
        name="write_out",
    )(error, q_mean)


def per_device(activations, output_grads, q_start):
    replicas = lax.axis_size("dp")
    shards = lax.axis_size("mp")
    tokens, depth = activations.shape
    gathered, width = output_grads.shape
    rank = q_start.shape[1]
    lines = rank // replicas
    span = depth // shards
    inner = gathered + 256
    dma = pltpu.SemaphoreType.DMA
    any_space = pl.BlockSpec(memory_space=pl.ANY)
    vmem = pl.BlockSpec(memory_space=pltpu.VMEM)
    error, q_mean = pl.pallas_call(
        functools.partial(step_kernel, (replicas, shards)),
        out_shape=(
            pltpu.VMEM((depth, width), BF16),
            jax.ShapeDtypeStruct((rank, width), F32),
        ),
        in_specs=[any_space, any_space, vmem],
        out_specs=(vmem, vmem),
        scratch_shapes=[
            pltpu.VMEM((inner, depth), BF16),
            pltpu.VMEM((inner, width), BF16),
            pltpu.VMEM((512, inner), BF16),
            pltpu.VMEM((shards, rank, tokens), F32),
            pltpu.VMEM((shards, rank, tokens), F32),
            pltpu.VMEM((replicas, lines, depth), F32),
            pltpu.VMEM((replicas, lines, depth), F32),
            pltpu.VMEM((replicas, lines, depth), F32),
            pltpu.VMEM((rank, depth), F32),
            pltpu.VMEM((shards, lines, span), F32),
            pltpu.VMEM((shards, lines, span), F32),
            pltpu.VMEM((shards, lines, span), F32),
            pltpu.VMEM((shards, rank, tokens), F32),
            dma((2,)),
        ]
        + [dma((shards,))] * 2
        + [dma((replicas,))] * 2
        + [dma((shards,))] * 4
        + [dma((replicas,))] * 2
        + [dma((shards,))] * 2
        + [dma((replicas,))] * 4
        + [dma((shards, CHUNKS))] * 4,
        compiler_params=pltpu.CompilerParams(
            collective_id=0, has_side_effects=True, vmem_limit_bytes=35 * 2**20
        ),
        name="step",
    )(activations, output_grads, q_start)
    return write_out(error, q_mean)


def solution(mesh):
    in_specs = (P(("dp", "mp"), None), P("dp", "mp"), P("mp", None))
    out_specs = (P("dp", "mp"), P("mp", None))
    return jax.shard_map(
        per_device, mesh=mesh, in_specs=in_specs, out_specs=out_specs, check_vma=False
    )
```

profile of v0, /device:TPU:0, one launch (start us, length us, event | category | flops | bytes accessed | tf_op | source)
XLA Modules:
  0.0 212.0 jit_solution(15752431355540918667)
XLA Ops:
  0.6 2.9 %copy.5.q_ref = f32[3584,64]{1,0:T(8,128)} copy(f32[3584,64]{0,1:T(8,128)} %param.5) | data formatting | bytes 1835008 | tf_op args[2]
  3.6 175.9 %step.1 = (bf16[4096,3584]{1,0:T(8,128)(2,1)S(1)}, f32[64,3584]{1,0:T(8,128)}) custom-call(bf16[256,4096]{1,0:T(8,128)(2,1)} %x_hbm.1, bf16[1024,3584]{1,0:T(8,128)(2,1)} %y_hbm.1, f32[3584,64]{1,0:T(8,128)} %copy.5.q_ref), custom_call_target="tpu_custom_call" | custom-call | tf_op jit(solution)/shard_map/step/pallas_call | solution.py:383
  179.4 0.0 copy-start
  179.5 10.3 %copy-done = bf16[4096,3584]{1,0:T(8,128)(2,1)} copy-done((bf16[4096,3584]{1,0:T(8,128)(2,1)}, bf16[4096,3584]{1,0:T(8,128)(2,1)S(1)}, u32[]{:S(2)}) %copy-start) | copy-done | bytes 29360152
  189.8 0.0 copy-start.1
  189.8 9.3 %copy-done.1 = bf16[4096,3584]{1,0:T(8,128)(2,1)S(1)} copy-done((bf16[4096,3584]{1,0:T(8,128)(2,1)S(1)}, bf16[4096,3584]{1,0:T(8,128)(2,1)}, u32[]{:S(2)}) %copy-start.1) | copy-done | bytes 29360152
  199.1 0.0 copy-start.2
  199.1 1.2 copy-done.2
  200.3 10.2 %write_out.1 = (bf16[4096,3584]{1,0:T(8,128)(2,1)}, f32[3584,64]{1,0:T(8,128)S(1)}) custom-call(bf16[4096,3584]{1,0:T(8,128)(2,1)S(1)} %copy-done.1, f32[64,3584]{1,0:T(8,128)S(1)} %copy-done.2), custom_call_target="tpu_custom_call" | custom-call | tf_op jit(solution)/shard_map/write_out/pallas_call | solution.py:357
  210.5 1.4 copy.6
Async XLA Ops:
  179.4 10.3 %copy-start = (bf16[4096,3584]{1,0:T(8,128)(2,1)}, bf16[4096,3584]{1,0:T(8,128)(2,1)S(1)}, u32[]{:S(2)}) copy-start(bf16[4096,3584]{1,0:T(8,128)(2,1)S(1)} %get-tuple-element.4.error_ref) | copy-start | bytes 88080384
  189.8 9.4 %copy-start.1 = (bf16[4096,3584]{1,0:T(8,128)(2,1)S(1)}, bf16[4096,3584]{1,0:T(8,128)(2,1)}, u32[]{:S(2)}) copy-start(bf16[4096,3584]{1,0:T(8,128)(2,1)} %copy-done) | copy-start | bytes 88080384
  199.1 1.2 copy-start.2
where the time goes:
time: 212 us
  Pallas kernels  186 us (88%)
  local copies, waits for them, and re-layouts  25.2 us (12%)
    pallas_call x1, Pallas kernels, per_device(): pl.pallas_call(functools.partial(step_kernel, (replicas, shards)), out_sh...  176 us
    unnamed x7, local copies, waits for them, and re-layouts  23.8 us
    pallas_call x1, Pallas kernels, write_out(): pl.pallas_call(write_kernel, out_shape=(jax.ShapeDtypeStruct((depth, widt...  10.2 us

commit v1 on v0

v1 whole, which is shorter than its diff:
```python
import functools

import jax
import jax.numpy as jnp
from jax import lax
from jax.experimental import pallas as pl
from jax.experimental.pallas import tpu as pltpu
from jax.sharding import PartitionSpec as P

ROWS = (((0,), (0,)), ((), ()))
COLS = (((1,), (1,)), ((), ()))
MESH = pl.DeviceIdType.MESH
F32 = jnp.float32
BF16 = jnp.bfloat16
CHUNKS = 16
EARLY = 14
EARLY_TILES = 5


def split_parts(values):
    upper = values.astype(BF16)
    lower = (values - upper.astype(F32)).astype(BF16)
    return (upper, lower)


def inverse_factor(gram):
    rank = gram.shape[0]
    row = lax.broadcasted_iota(jnp.int32, (rank, rank), 0)
    col = lax.broadcasted_iota(jnp.int32, (rank, rank), 1)
    left = gram
    right = jnp.where(row == col, 1.0, 0.0).astype(F32)
    down = lax.broadcasted_iota(jnp.int32, (rank, 1), 0)
    pivots = jnp.ones((rank, 1), F32)
    for k in range(rank):
        pivot = left[k : k + 1, k : k + 1]
        pivots = jnp.where(down == k, pivot, pivots)
        factor = jnp.where(down > k, left[:, k : k + 1] / pivot, 0.0)
        left_row = left[k : k + 1, :]
        right_row = right[k : k + 1, :]
        left = left - factor * left_row
        right = right - factor * right_row
    return right / jnp.sqrt(pivots)


class Exchange:
    def __init__(self, axis, count, me, source, target, send_sem, recv_sem):
        self.copies = []
        for shift in range(1, count):
            peer = lax.rem(me + shift, count)
            self.copies.append(
                pltpu.make_async_remote_copy(
                    src_ref=source(peer),
                    dst_ref=target,
                    send_sem=send_sem.at[shift],
                    recv_sem=recv_sem.at[shift],
                    device_id={axis: peer},
                    device_id_type=MESH,
                )
            )

    def start(self):
        for copy in self.copies:
            copy.start()

    def wait(self):
        for copy in self.copies:
            copy.wait()


def step_kernel(
    dims,
    x_hbm,
    y_hbm,
    q_ref,
    e_ref,
    q_out,
    xg,
    yv,
    xown,
    pcat,
    zpart,
    zrecv,
    part,
    recv,
    full,
    pmat,
    psum,
    pzr,
    pz,
    wall,
    upart,
    urecv,
    ufull,
    local_sem,
    zs_sem,
    zr_sem,
    ps_sem,
    pr_sem,
    pzs_sem,
    pzr_sem,
    ags_sem,
    agr_sem,
    pgs_sem,
    pgr_sem,
    ws_sem,
    wr_sem,
    us_sem,
    ur_sem,
    uas_sem,
    uar_sem,
    right_send,
    right_recv,
    left_send,
    left_recv,
):
    replicas, shards = dims
    me = lax.axis_index("mp")
    rep = lax.axis_index("dp")
    tokens, depth = x_hbm.shape
    gathered, width = y_hbm.shape
    rank = q_ref.shape[0]
    lines = rank // replicas
    span = depth // shards
    chunk = depth // CHUNKS
    highest = lax.Precision.HIGHEST

    x_copy = pltpu.make_async_copy(x_hbm, xown, local_sem.at[0])
    y_copy = pltpu.make_async_copy(y_hbm, yv.at[pl.ds(0, gathered), :], local_sem.at[1])
    x_copy.start()
    y_copy.start()

    barrier = pltpu.get_barrier_semaphore()
    for shift in range(1, shards):
        peer = lax.rem(me + shift, shards)
        pl.semaphore_signal(barrier, inc=1, device_id={"mp": peer}, device_id_type=MESH)
    for shift in range(1, replicas):
        peer = lax.rem(rep + shift, replicas)
        pl.semaphore_signal(barrier, inc=1, device_id={"dp": peer}, device_id_type=MESH)
    pl.semaphore_wait(barrier, shards + replicas - 2)

    def hop(owner, c, send_sem, recv_sem, target):
        block = xg.at[owner, pl.ds(pl.multiple_of(c * chunk, chunk), chunk), :]
        return pltpu.make_async_remote_copy(
            src_ref=block,
            dst_ref=block,
            send_sem=send_sem,
            recv_sem=recv_sem,
            device_id={"mp": target},
            device_id_type=MESH,
        )

    def turn(c):
        if c < CHUNKS:
            cols = pl.ds(c * chunk, chunk)
            xg[me, cols, :] = xown[:, cols].T

    def relay(step):
        turn(step + 1)
        for h in range(shards):
            c = step - h
            inside = jnp.logical_and(c >= 0, c < CHUNKS)
            for ahead, sends, recvs in ((True, right_send, right_recv), (False, left_send, left_recv)):
                owner = me - h if ahead else me + h
                exists = owner >= 0 if ahead else owner < shards
                onward = me < shards - 1 if ahead else me > 0
                target = me + 1 if ahead else me - 1
                source = me - 1 if ahead else me + 1
                if h >= 1:

                    @pl.when(jnp.logical_and(inside, exists))
                    def _():
                        hop(owner, c, sends.at[h - 1, c], recvs.at[h - 1, c], source).wait_recv()

                if h < shards - 1:

                    @pl.when(jnp.logical_and(inside, jnp.logical_and(exists, onward)))
                    def _():
                        hop(owner, c, sends.at[h, c], recvs.at[h, c], target).start()

    tall = 2 * chunk
    wide = width // 2
    blocks = range(shards)

    def sweep(body):
        def column(n, carry):
            body(pl.ds(pl.multiple_of(n * wide, wide), wide))
            return carry

        lax.fori_loop(0, width // wide, column, 0)

    def draft(first, size):
        rows = pl.ds(first, size)

        def body(cols):
            lhs = jnp.concatenate([xg[b, rows, :] for b in blocks], axis=1)
            e_ref[rows, cols] = jnp.dot(
                lhs, yv[pl.ds(0, gathered), cols], preferred_element_type=F32
            ).astype(BF16)

        sweep(body)

    def patch(first, size):
        rows = pl.ds(first, size)

        def body(cols):
            low = jnp.dot(
                pcat[rows, :], yv[pl.ds(gathered, inner), cols], preferred_element_type=F32
            )
            e_ref[rows, cols] = (e_ref[rows, cols].astype(F32) + low).astype(BF16)

        sweep(body)

    def tile(first, size):
        rows = pl.ds(first, size)

        def body(cols):
            lhs = jnp.concatenate([xg[b, rows, :] for b in blocks] + [pcat[rows, :]], axis=1)
            e_ref[rows, cols] = jnp.dot(lhs, yv[:, cols], preferred_element_type=F32).astype(BF16)

        sweep(body)

    x_copy.wait()
    turn(0)
    relay(0)

    q_cat = jnp.concatenate(split_parts(q_ref[...]), axis=0)
    inner = yv.shape[0] - gathered
    yv[pl.ds(gathered + 2 * rank, inner - 2 * rank), :] = jnp.zeros((inner - 2 * rank, width), BF16)
    y_copy.wait()
    both = lax.dot_general(yv[pl.ds(0, gathered), :], q_cat, COLS, preferred_element_type=F32)
    both = both.T
    projected = both[:rank] + both[rank:]
    for j in range(shards):
        zpart[j] = projected[:, j * tokens : (j + 1) * tokens].astype(zpart.dtype)
    z_move = Exchange("mp", shards, me, lambda peer: zpart.at[peer], zrecv.at[me], zs_sem, zr_sem)
    z_move.start()
    relay(1)
    z_move.wait()
    total = zpart[me].astype(F32)
    for shift in range(1, shards):
        total = total + zrecv[lax.rem(me + shift, shards)].astype(F32)

    z_cat = jnp.concatenate(split_parts(total), axis=0)
    both = jnp.dot(z_cat, xown[...], preferred_element_type=F32)
    left = both[:rank] + both[rank:]
    for i in range(replicas):
        part[i] = left[i * lines : (i + 1) * lines, :]
    p_move = Exchange("dp", replicas, rep, lambda peer: part.at[peer], recv.at[rep], ps_sem, pr_sem)
    p_move.start()
    relay(2)
    relay(3)
    p_move.wait()
    total = part[rep]
    for shift in range(1, replicas):
        total = total + recv[lax.rem(rep + shift, replicas)]
    for j in range(shards):
        psum[j] = total[:, j * span : (j + 1) * span]
    pz_move = Exchange("mp", shards, me, lambda peer: psum.at[peer], pzr.at[me], pzs_sem, pzr_sem)
    pz_move.start()
    relay(4)
    pz_move.wait()
    total = psum[me]
    for shift in range(1, shards):
        total = total + pzr[lax.rem(me + shift, shards)]
    pz[me] = total / replicas
    ag_move = Exchange("mp", shards, me, lambda peer: pz.at[me], pz.at[me], ags_sem, agr_sem)
    ag_move.start()
    relay(5)
    ag_move.wait()
    for j in range(shards):
        full[rep, :, pl.ds(j * span, span)] = pz[j]
    pg_move = Exchange("dp", replicas, rep, lambda peer: full.at[rep], full.at[rep], pgs_sem, pgr_sem)
    pg_move.start()
    relay(6)
    draft(0, tall)
    relay(7)
    pg_move.wait()
    for i in range(replicas):
        pmat[pl.ds(i * lines, lines), :] = full[i]
    relay(8)
    draft(tall, tall)

    p_mean = pmat[...]
    gram = lax.dot_general(p_mean, p_mean, COLS, precision=highest, preferred_element_type=F32)
    inverse = inverse_factor(gram)
    ortho = jnp.dot(inverse, pmat[...], precision=highest, preferred_element_type=F32)
    ortho_cat = jnp.concatenate(split_parts(-ortho), axis=0)

    both = lax.dot_general(ortho_cat, xown[...], COLS, preferred_element_type=F32)
    wall[me] = -(both[:rank] + both[rank:]).astype(wall.dtype)
    w_move = Exchange("mp", shards, me, lambda peer: wall.at[me], wall.at[me], ws_sem, wr_sem)
    w_move.start()
    pcat[:, pl.ds(0, 2 * rank)] = ortho_cat.T
    pcat[:, pl.ds(2 * rank, inner - 2 * rank)] = jnp.zeros((depth, inner - 2 * rank), BF16)
    relay(9)
    w_move.wait()
    seen = jnp.concatenate([wall[j] for j in range(shards)], axis=1)
    right = jnp.dot(seen, yv[pl.ds(0, gathered), :], preferred_element_type=F32)
    used = pl.ds(0, width)
    for i in range(replicas):
        upart[i] = right[i * lines : (i + 1) * lines, :].astype(BF16)
    u_move = Exchange("dp", replicas, rep, lambda peer: upart.at[peer], urecv.at[rep], us_sem, ur_sem)
    u_move.start()
    relay(10)
    draft(2 * tall, tall)
    relay(11)
    u_move.wait()
    total = upart[rep].astype(F32)
    for shift in range(1, replicas):
        total = total + urecv[lax.rem(rep + shift, replicas)].astype(F32)
    ufull[rep] = (total / replicas).astype(BF16)
    ua_move = Exchange("dp", replicas, rep, lambda peer: ufull.at[rep], ufull.at[rep], uas_sem, uar_sem)
    ua_move.start()
    relay(12)
    draft(3 * tall, tall)
    relay(13)
    draft(4 * tall, tall)
    ua_move.wait()
    for i in range(replicas):
        pmat[pl.ds(i * lines, lines), used] = ufull[i].astype(F32)
    q_mean = pmat[:, used]
    q_out[...] = q_mean
    upper = q_mean.astype(BF16)
    yv[pl.ds(gathered, rank), :] = upper
    yv[pl.ds(gathered + rank, rank), :] = upper

    for t in range(EARLY_TILES):
        patch(t * tall, tall)
    halves = CHUNKS // 2
    last = CHUNKS + shards - 1
    done = EARLY
    for t in range(EARLY_TILES, halves - 1):
        for step in range(done, 2 * t + shards + 1):
            relay(step)
        done = max(done, 2 * t + shards + 1)
        tile(t * tall, tall)
    for t in (CHUNKS - 2, CHUNKS - 1):
        for step in range(done, t + shards):
            relay(step)
        done = max(done, t + shards)
        tile(t * chunk, chunk)

    def drain(c, carry):
        for h in range(shards - 1):

            @pl.when(jnp.logical_and(me - h >= 0, me < shards - 1))
            def _():
                hop(me - h, c, right_send.at[h, c], right_recv.at[h, c], me + 1).wait_send()

            @pl.when(jnp.logical_and(me + h < shards, me > 0))
            def _():
                hop(me + h, c, left_send.at[h, c], left_recv.at[h, c], me - 1).wait_send()

        return carry

    lax.fori_loop(0, CHUNKS, drain, 0)


def write_kernel(error_ref, q_ref, error_out, q_out, sem):
    parts = sem.shape[0] - 1
    rows = error_ref.shape[0] // parts
    copies = []
    for k in range(parts):
        here = pl.ds(k * rows, rows)
        copies.append(
            pltpu.make_async_copy(error_ref.at[here, :], error_out.at[here, :], sem.at[k])
        )
        copies[-1].start()
    q_copy = pltpu.make_async_copy(q_ref, q_out, sem.at[parts])
    q_copy.start()
    for copy in copies:
        copy.wait()
    q_copy.wait()


def write_out(error, q_mean):
    vmem = pl.BlockSpec(memory_space=pltpu.VMEM)
    hbm = pl.BlockSpec(memory_space=pl.ANY)
    return pl.pallas_call(
        write_kernel,
        out_shape=(
            jax.ShapeDtypeStruct(error.shape, error.dtype),
            jax.ShapeDtypeStruct(q_mean.shape, q_mean.dtype),
        ),
        in_specs=[vmem, vmem],
        out_specs=(hbm, hbm),
        scratch_shapes=[pltpu.SemaphoreType.DMA((9,))],
        compiler_params=pltpu.CompilerParams(vmem_limit_bytes=2 * 2**20),
        name="write_out",
    )(error, q_mean)


def per_device(activations, output_grads, q_start):
    replicas = lax.axis_size("dp")
    shards = lax.axis_size("mp")
    tokens, depth = activations.shape
    gathered, width = output_grads.shape
    rank = q_start.shape[1]
    lines = rank // replicas
    span = depth // shards
    inner = 256
    dma = pltpu.SemaphoreType.DMA
    any_space = pl.BlockSpec(memory_space=pl.ANY)
    vmem = pl.BlockSpec(memory_space=pltpu.VMEM)
    error, q_mean = pl.pallas_call(
        functools.partial(step_kernel, (replicas, shards)),
        out_shape=(
            pltpu.VMEM((depth, width), BF16),
            pltpu.VMEM((rank, width), F32),
        ),
        in_specs=[any_space, any_space, vmem],
        out_specs=(vmem, vmem),
        scratch_shapes=[
            pltpu.VMEM((shards, depth, tokens), BF16),
            pltpu.VMEM((gathered + inner, width), BF16),
            pltpu.VMEM((tokens, depth), BF16),
            pltpu.VMEM((depth, inner), BF16),
            pltpu.VMEM((shards, rank, tokens), BF16),
            pltpu.VMEM((shards, rank, tokens), BF16),
            pltpu.VMEM((replicas, lines, depth), F32),
            pltpu.VMEM((replicas, lines, depth), F32),
            pltpu.VMEM((replicas, lines, depth), F32),
            pltpu.VMEM((rank, depth), F32),
            pltpu.VMEM((shards, lines, span), F32),
            pltpu.VMEM((shards, lines, span), F32),
            pltpu.VMEM((shards, lines, span), F32),
            pltpu.VMEM((shards, rank, tokens), BF16),
            pltpu.VMEM((replicas, lines, width), BF16),
            pltpu.VMEM((replicas, lines, width), BF16),
            pltpu.VMEM((replicas, lines, width), BF16),
            dma((2,)),
        ]
        + [dma((shards,))] * 2
        + [dma((replicas,))] * 2
        + [dma((shards,))] * 4
        + [dma((replicas,))] * 2
        + [dma((shards,))] * 2
        + [dma((replicas,))] * 4
        + [dma((shards, CHUNKS))] * 4,
        compiler_params=pltpu.CompilerParams(
            collective_id=0, has_side_effects=True, vmem_limit_bytes=34 * 2**20
        ),
        name="step",
    )(activations, output_grads, q_start.T)
    error, q_mean = write_out(error, q_mean)
    return (error, q_mean.T)


def solution(mesh):
    in_specs = (P(("dp", "mp"), None), P("dp", "mp"), P("mp", None))
    out_specs = (P("dp", "mp"), P("mp", None))
    return jax.shard_map(
        per_device, mesh=mesh, in_specs=in_specs, out_specs=out_specs, check_vma=False
    )
```

time: 212 us -> 174 us (0.82)
  local copies, waits for them, and re-layouts: 25.2 us -> 0 us
  Pallas kernels: 186 us -> 173 us
    unnamed x7 -> x0, local copies, waits for them, and re-layouts: 23.8 us -> none
    pallas_call x1, Pallas kernels: 176 us -> 163 us  [per_device(): pl.pallas_call(functools.partial(step_kernel, (replicas, shards)), out_sh...]
where the time goes in v1:
time: 174 us; the launch traced here: 173 us
  Pallas kernels  173 us (99%)
    pallas_call x1, Pallas kernels, per_device(): pl.pallas_call(functools.partial(step_kernel, (replicas, shards)), out_sh...  163 us
    pallas_call x1, Pallas kernels, write_out(): pl.pallas_call(write_kernel, out_shape=(jax.ShapeDtypeStruct(error.shape,...  10 us

profile of v1, /device:TPU:0, one launch (start us, length us, event | category | flops | bytes accessed | tf_op | source)
XLA Modules:
  0.0 173.4 jit_solution(4894171114588799561)
XLA Ops:
  0.6 162.6 %step.1 = (bf16[4096,3584]{1,0:T(8,128)(2,1)S(1)}, f32[64,3584]{1,0:T(8,128)S(1)}) custom-call(bf16[256,4096]{1,0:T(8,128)(2,1)} %x_hbm.1, bf16[1024,3584]{1,0:T(8,128)(2,1)} %y_hbm.1, f32[64,3584]{1,0:T(8,128)} %bitcast.2), custom_call_target="tpu_custom_call" | custom-call | tf_op jit(solution)/shard_map/step/pallas_call | solution.py:405
  163.2 10.0 %write_out.1 = (bf16[4096,3584]{1,0:T(8,128)(2,1)}, f32[64,3584]{1,0:T(8,128)}) custom-call(bf16[4096,3584]{1,0:T(8,128)(2,1)S(1)} %get-tuple-element.6.error_ref, f32[64,3584]{1,0:T(8,128)S(1)} %get-tuple-element.7.q_ref), custom_call_target="tpu_custom_call" | custom-call | tf_op jit(solution)/shard_map/write_out/pallas_call | solution.py:379

commit v2 on v1

--- a/solution.py
+++ b/solution.py
@@ -13,8 +13,6 @@
 F32 = jnp.float32
 BF16 = jnp.bfloat16
 CHUNKS = 16
-EARLY = 14
-EARLY_TILES = 5
 
 
 def split_parts(values):
@@ -23,7 +21,7 @@
     return (upper, lower)
 
 
-def inverse_factor(gram):
+def inverse_factor(gram, between):
     rank = gram.shape[0]
     row = lax.broadcasted_iota(jnp.int32, (rank, rank), 0)
     col = lax.broadcasted_iota(jnp.int32, (rank, rank), 1)
@@ -34,6 +32,8 @@
     for k in range(rank):
         pivot = left[k : k + 1, k : k + 1]
         pivots = jnp.where(down == k, pivot, pivots)
+        if k == rank // 2:
+            between()
         factor = jnp.where(down > k, left[:, k : k + 1] / pivot, 0.0)
         left_row = left[k : k + 1, :]
         right_row = right[k : k + 1, :]
@@ -122,6 +122,7 @@
     lines = rank // replicas
     span = depth // shards
     chunk = depth // CHUNKS
+    tall = 2 * chunk
     highest = lax.Precision.HIGHEST
 
     x_copy = pltpu.make_async_copy(x_hbm, xown, local_sem.at[0])
@@ -155,29 +156,54 @@
             xg[me, cols, :] = xown[:, cols].T
 
     def relay(step):
-        turn(step + 1)
-        for h in range(shards):
-            c = step - h
-            inside = jnp.logical_and(c >= 0, c < CHUNKS)
+        turn(step + 2)
+        for h in range(shards - 1):
+            c = step + 1 if h == 0 else step - h
+            if c < 0 or c >= CHUNKS:
+                continue
             for ahead, sends, recvs in ((True, right_send, right_recv), (False, left_send, left_recv)):
                 owner = me - h if ahead else me + h
                 exists = owner >= 0 if ahead else owner < shards
                 onward = me < shards - 1 if ahead else me > 0
                 target = me + 1 if ahead else me - 1
                 source = me - 1 if ahead else me + 1
-                if h >= 1:
-
-                    @pl.when(jnp.logical_and(inside, exists))
-                    def _():
+
+                @pl.when(jnp.logical_and(exists, onward))
+                def _():
+                    if h >= 1:
                         hop(owner, c, sends.at[h - 1, c], recvs.at[h - 1, c], source).wait_recv()
-
-                if h < shards - 1:
-
-                    @pl.when(jnp.logical_and(inside, jnp.logical_and(exists, onward)))
-                    def _():
-                        hop(owner, c, sends.at[h, c], recvs.at[h, c], target).start()
-
-    tall = 2 * chunk
+                    hop(owner, c, sends.at[h, c], recvs.at[h, c], target).start()
+
+    def arrive(c):
+        @pl.when(me == shards - 1)
+        def _():
+            for h in range(1, shards):
+                hop(me - h, c, right_send.at[h - 1, c], right_recv.at[h - 1, c], me - 1).wait_recv()
+
+        @pl.when(me == 0)
+        def _():
+            for h in range(1, shards):
+                hop(me + h, c, left_send.at[h - 1, c], left_recv.at[h - 1, c], me + 1).wait_recv()
+
+    state = {"relay": -1, "draft": 0}
+    halves = CHUNKS // 2
+    last = CHUNKS + shards - 2
+
+    def advance(count):
+        for _ in range(count):
+            if state["relay"] < last:
+                relay(state["relay"])
+                state["relay"] += 1
+
+    def early(count):
+        for _ in range(count):
+            t = state["draft"]
+            if t < halves - 1 and 2 * t + shards < state["relay"]:
+                arrive(2 * t)
+                arrive(2 * t + 1)
+                draft(t * tall, tall)
+                state["draft"] += 1
+
     wide = width // 2
     blocks = range(shards)
 
@@ -221,11 +247,12 @@
 
     x_copy.wait()
     turn(0)
-    relay(0)
+    turn(1)
+    advance(2)
 
     q_cat = jnp.concatenate(split_parts(q_ref[...]), axis=0)
     inner = yv.shape[0] - gathered
-    yv[pl.ds(gathered + 2 * rank, inner - 2 * rank), :] = jnp.zeros((inner - 2 * rank, width), BF16)
+    yv[pl.ds(gathered + 3 * rank, inner - 3 * rank), :] = jnp.zeros((inner - 3 * rank, width), BF16)
     y_copy.wait()
     both = lax.dot_general(yv[pl.ds(0, gathered), :], q_cat, COLS, preferred_element_type=F32)
     both = both.T
@@ -234,7 +261,7 @@
         zpart[j] = projected[:, j * tokens : (j + 1) * tokens].astype(zpart.dtype)
     z_move = Exchange("mp", shards, me, lambda peer: zpart.at[peer], zrecv.at[me], zs_sem, zr_sem)
     z_move.start()
-    relay(1)
+    advance(1)
     z_move.wait()
     total = zpart[me].astype(F32)
     for shift in range(1, shards):
@@ -247,42 +274,40 @@
         part[i] = left[i * lines : (i + 1) * lines, :]
     p_move = Exchange("dp", replicas, rep, lambda peer: part.at[peer], recv.at[rep], ps_sem, pr_sem)
     p_move.start()
-    relay(2)
-    relay(3)
+    advance(2)
     p_move.wait()
     total = part[rep]
     for shift in range(1, replicas):
         total = total + recv[lax.rem(rep + shift, replicas)]
     for j in range(shards):
-        psum[j] = total[:, j * span : (j + 1) * span]
+        psum[j] = total[:, j * span : (j + 1) * span].astype(BF16)
     pz_move = Exchange("mp", shards, me, lambda peer: psum.at[peer], pzr.at[me], pzs_sem, pzr_sem)
     pz_move.start()
-    relay(4)
+    advance(1)
     pz_move.wait()
-    total = psum[me]
+    total = psum[me].astype(F32)
     for shift in range(1, shards):
-        total = total + pzr[lax.rem(me + shift, shards)]
-    pz[me] = total / replicas
+        total = total + pzr[lax.rem(me + shift, shards)].astype(F32)
+    pz[me] = (total / replicas).astype(BF16)
     ag_move = Exchange("mp", shards, me, lambda peer: pz.at[me], pz.at[me], ags_sem, agr_sem)
     ag_move.start()
-    relay(5)
+    advance(1)
     ag_move.wait()
     for j in range(shards):
-        full[rep, :, pl.ds(j * span, span)] = pz[j]
+        full[rep, :, pl.ds(j * span, span)] = pz[j].astype(F32)
     pg_move = Exchange("dp", replicas, rep, lambda peer: full.at[rep], full.at[rep], pgs_sem, pgr_sem)
     pg_move.start()
-    relay(6)
-    draft(0, tall)
-    relay(7)
+    advance(1)
+    early(1)
+    advance(1)
     pg_move.wait()
     for i in range(replicas):
         pmat[pl.ds(i * lines, lines), :] = full[i]
-    relay(8)
-    draft(tall, tall)
+    advance(1)
 
     p_mean = pmat[...]
     gram = lax.dot_general(p_mean, p_mean, COLS, precision=highest, preferred_element_type=F32)
-    inverse = inverse_factor(gram)
+    inverse = inverse_factor(gram, lambda: advance(1))
     ortho = jnp.dot(inverse, pmat[...], precision=highest, preferred_element_type=F32)
     ortho_cat = jnp.concatenate(split_parts(-ortho), axis=0)
 
@@ -290,54 +315,54 @@
     wall[me] = -(both[:rank] + both[rank:]).astype(wall.dtype)
     w_move = Exchange("mp", shards, me, lambda peer: wall.at[me], wall.at[me], ws_sem, wr_sem)
     w_move.start()
-    pcat[:, pl.ds(0, 2 * rank)] = ortho_cat.T
-    pcat[:, pl.ds(2 * rank, inner - 2 * rank)] = jnp.zeros((depth, inner - 2 * rank), BF16)
-    relay(9)
+    turned = ortho_cat.T
+    pcat[:, pl.ds(0, 2 * rank)] = turned
+    pcat[:, pl.ds(2 * rank, rank)] = turned[:, :rank]
+    pcat[:, pl.ds(3 * rank, inner - 3 * rank)] = jnp.zeros((depth, inner - 3 * rank), BF16)
+    early(1)
+    advance(1)
     w_move.wait()
     seen = jnp.concatenate([wall[j] for j in range(shards)], axis=1)
     right = jnp.dot(seen, yv[pl.ds(0, gathered), :], preferred_element_type=F32)
     used = pl.ds(0, width)
     for i in range(replicas):
-        upart[i] = right[i * lines : (i + 1) * lines, :].astype(BF16)
+        upart[i] = right[i * lines : (i + 1) * lines, :]
     u_move = Exchange("dp", replicas, rep, lambda peer: upart.at[peer], urecv.at[rep], us_sem, ur_sem)
     u_move.start()
-    relay(10)
-    draft(2 * tall, tall)
-    relay(11)
+    advance(1)
+    early(1)
+    advance(1)
     u_move.wait()
-    total = upart[rep].astype(F32)
+    total = upart[rep]
     for shift in range(1, replicas):
-        total = total + urecv[lax.rem(rep + shift, replicas)].astype(F32)
-    ufull[rep] = (total / replicas).astype(BF16)
+        total = total + urecv[lax.rem(rep + shift, replicas)]
+    ufull[rep] = total / replicas
     ua_move = Exchange("dp", replicas, rep, lambda peer: ufull.at[rep], ufull.at[rep], uas_sem, uar_sem)
     ua_move.start()
-    relay(12)
-    draft(3 * tall, tall)
-    relay(13)
-    draft(4 * tall, tall)
+    advance(1)
+    early(1)
+    advance(1)
+    early(1)
     ua_move.wait()
     for i in range(replicas):
-        pmat[pl.ds(i * lines, lines), used] = ufull[i].astype(F32)
+        pmat[pl.ds(i * lines, lines), used] = ufull[i]
     q_mean = pmat[:, used]
     q_out[...] = q_mean
-    upper = q_mean.astype(BF16)
+    upper, lower = split_parts(q_mean)
     yv[pl.ds(gathered, rank), :] = upper
     yv[pl.ds(gathered + rank, rank), :] = upper
-
-    for t in range(EARLY_TILES):
+    yv[pl.ds(gathered + 2 * rank, rank), :] = lower
+    advance(1)
+    for t in range(state["draft"]):
         patch(t * tall, tall)
-    halves = CHUNKS // 2
-    last = CHUNKS + shards - 1
-    done = EARLY
-    for t in range(EARLY_TILES, halves - 1):
-        for step in range(done, 2 * t + shards + 1):
-            relay(step)
-        done = max(done, 2 * t + shards + 1)
+        advance(1)
+    advance(last)
+    for t in range(state["draft"], halves - 1):
+        arrive(2 * t)
+        arrive(2 * t + 1)
         tile(t * tall, tall)
     for t in (CHUNKS - 2, CHUNKS - 1):
-        for step in range(done, t + shards):
-            relay(step)
-        done = max(done, t + shards)
+        arrive(t)
         tile(t * chunk, chunk)
 
     def drain(c, carry):
@@ -421,13 +446,13 @@
             pltpu.VMEM((replicas, lines, depth), F32),
             pltpu.VMEM((replicas, lines, depth), F32),
             pltpu.VMEM((rank, depth), F32),
-            pltpu.VMEM((shards, lines, span), F32),
-            pltpu.VMEM((shards, lines, span), F32),
-            pltpu.VMEM((shards, lines, span), F32),
+            pltpu.VMEM((shards, lines, span), BF16),
+            pltpu.VMEM((shards, lines, span), BF16),
+            pltpu.VMEM((shards, lines, span), BF16),
             pltpu.VMEM((shards, rank, tokens), BF16),
-            pltpu.VMEM((replicas, lines, width), BF16),
-            pltpu.VMEM((replicas, lines, width), BF16),
-            pltpu.VMEM((replicas, lines, width), BF16),
+            pltpu.VMEM((replicas, lines, width), F32),
+            pltpu.VMEM((replicas, lines, width), F32),
+            pltpu.VMEM((replicas, lines, width), F32),
             dma((2,)),
         ]
         + [dma((shards,))] * 2

time: 174 us -> 167 us (0.960)
  Pallas kernels: 173 us -> 166 us
    pallas_call x1, Pallas kernels: 163 us -> 156 us  [per_device(): pl.pallas_call(functools.partial(step_kernel, (replicas, shards)), out_sh...]
where the time goes in v2:
time: 167 us
  Pallas kernels  166 us (99%)
    pallas_call x1, Pallas kernels, per_device(): pl.pallas_call(functools.partial(step_kernel, (replicas, shards)), out_sh...  156 us
    pallas_call x1, Pallas kernels, write_out(): pl.pallas_call(write_kernel, out_shape=(jax.ShapeDtypeStruct(error.shape,...  10 us

profile of v2, /device:TPU:0, one launch (start us, length us, event | category | flops | bytes accessed | tf_op | source)
XLA Modules:
  0.0 166.5 jit_solution(6956553491913869973)
XLA Ops:
  0.6 155.7 %step.1 = (bf16[4096,3584]{1,0:T(8,128)(2,1)S(1)}, f32[64,3584]{1,0:T(8,128)S(1)}) custom-call(bf16[256,4096]{1,0:T(8,128)(2,1)} %x_hbm.1, bf16[1024,3584]{1,0:T(8,128)(2,1)} %y_hbm.1, f32[64,3584]{1,0:T(8,128)} %bitcast.2), custom_call_target="tpu_custom_call" | custom-call | tf_op jit(solution)/shard_map/step/pallas_call | solution.py:430
  156.3 10.0 %write_out.1 = (bf16[4096,3584]{1,0:T(8,128)(2,1)}, f32[64,3584]{1,0:T(8,128)}) custom-call(bf16[4096,3584]{1,0:T(8,128)(2,1)S(1)} %get-tuple-element.6.error_ref, f32[64,3584]{1,0:T(8,128)S(1)} %get-tuple-element.7.q_ref), custom_call_target="tpu_custom_call" | custom-call | tf_op jit(solution)/shard_map/write_out/pallas_call | solution.py:404
